TPU v7x, 32 devices: a whole 2x2x4 slice. The times are simulated.
32 devices in a mesh: lat: 4 (over y, core), lon: 8 (over z, x).
Axes of the slice: x: 2, y: 2, z: 4, core: 2. Of those that a mesh axis runs over, the one named last changes fastest.
Arguments:
- forcing: float32 [640, 1024], P('lat', 'lon'), may hold values from -28 to 28
- search_direction: float32 [640, 1024], P('lat', 'lon'), may hold values from -28 to 28
- ocean_depth: float32 [640, 1024], P('lat', 'lon'), may hold values from 0.5 to 8
- land_mask: int32 [640, 1024], P('lat', 'lon'), may hold values 0 or 1
- fold_map: int32 [1024], replicated, may hold values from 0 to 1023, as said below
Outputs:
- scaled_height: float32 [640, 1024], P('lat', 'lon')
- residual: float32 [640, 1024], P('lat', 'lon')
Inputs may be any that keep to these rules, and one draw needn't show every extreme that they name: `fold_map`: column j's partner across the fold is (c - j) mod 1024 for one c of 0 to 1023, so the map is its own inverse.
All inputs are finite; a program needn't handle non-finite values. No bound on the sum of `land_mask` on one device may be relied on, other than what follows from the above.
Results may differ from a plain program's by a relative error of at most 0.0003.
Values sent between devices are 32-bit elements; how exact they have to be, the bound alone decides.
A program may use at most 64 MiB of HBM per device.

v0:
```python
import jax
import jax.numpy as jnp
import numpy as np
from jax import lax
from jax.sharding import PartitionSpec as P

STEPS = 8
REACH = 256


PRECISE = lax.Precision.HIGHEST
DIRECTIONS = ((1, 0), (-1, 0), (0, 1), (0, -1), (1, 1), (-1, -1), (1, -1), (-1, 1))
LINK_FACTORS = (1.0, 1.0, 1.0, 1.0, 0.5, 0.5, 0.5, 0.5)


def with_halo(x, sides, width):
    for axis, dim in sides:
        size, length = (lax.axis_size(axis), x.shape[dim])
        up = [(i, (i + 1) % size) for i in range(size)]
        down = [(j, i) for i, j in up]
        last = lax.slice_in_dim(x, length - width, length, axis=dim)
        leading = lax.slice_in_dim(x, 0, width, axis=dim)
        before = lax.ppermute(last, axis, up)
        after = lax.ppermute(leading, axis, down)
        x = jnp.concatenate([before, x, after], axis=dim)
    return x


def chebyshev_table(basis_steps):
    number = 2 * basis_steps + 1
    matrix = np.zeros((number, number), np.float32)
    for offset, length in ((0, basis_steps + 1), (basis_steps + 1, basis_steps)):
        for column in range(length - 1):
            matrix[offset + column, offset + column] = 1.0
            if column == 0:
                matrix[offset + 1, offset] = 1.0
            else:
                matrix[offset + column + 1, offset + column] = 0.5
                matrix[offset + column - 1, offset + column] = 0.5
    return matrix


def coordinates(gram_matrix, basis_steps):
    number = 2 * basis_steps + 1
    shift_matrix = jnp.asarray(chebyshev_table(basis_steps))
    unit_rows = jnp.eye(number, dtype=jnp.float32)
    solution_coords = jnp.zeros((number,), jnp.float32)
    direction_coords = unit_rows[0]
    residual_coords = unit_rows[basis_steps + 1]
    norm_now = jnp.dot(
        residual_coords, jnp.dot(gram_matrix, residual_coords, precision=PRECISE), precision=PRECISE
    )
    for inner_step in range(basis_steps):
        mapped = jnp.dot(shift_matrix, direction_coords, precision=PRECISE)
        curvature = jnp.dot(
            direction_coords, jnp.dot(gram_matrix, mapped, precision=PRECISE), precision=PRECISE
        )
        step_length = norm_now / curvature
        solution_coords = solution_coords + step_length * direction_coords
        residual_coords = residual_coords - step_length * mapped
        norm_next = jnp.dot(
            residual_coords,
            jnp.dot(gram_matrix, residual_coords, precision=PRECISE),
            precision=PRECISE,
        )
        direction_coords = residual_coords + norm_next / norm_now * direction_coords
        norm_now = norm_next
    return (solution_coords, residual_coords, direction_coords)


def trim_margin(source, margin_cells):
    if margin_cells == 0:
        return source
    return source[
        ...,
        margin_cells : source.shape[-2] - margin_cells,
        margin_cells : source.shape[-1] - margin_cells,
    ]


def place_fold(widened, fold_rows, fold_map, margin_cells):
    lat_count = lax.axis_size("lat")
    lat_place = lax.axis_index("lat")
    lon_width = widened.shape[-1] - 2 * margin_cells
    total_columns = fold_map.shape[0]
    columns = (
        lax.axis_index("lon") * lon_width
        - margin_cells
        + jnp.arange(lon_width + 2 * margin_cells, dtype=jnp.int32)
    ) % total_columns
    partners = jnp.take(fold_map, columns)
    mirrored = jnp.take(fold_rows[:, ::-1, :], partners, axis=2)
    north_rows = jnp.where(
        lat_place == lat_count - 1, mirrored, widened[:, widened.shape[1] - margin_cells :, :]
    )
    south_rows = jnp.where(lat_place == 0, 0.0, widened[:, :margin_cells, :])
    return jnp.concatenate(
        [south_rows, widened[:, margin_cells : widened.shape[1] - margin_cells, :], north_rows],
        axis=1,
    )


def extend_depth(fields, fold_map, margin_cells):
    widened = with_halo(fields, (("lat", 1), ("lon", 2)), margin_cells)
    fold_rows = lax.all_gather(
        fields[:, fields.shape[1] - margin_cells :, :], "lon", axis=2, tiled=True
    )
    return place_fold(widened, fold_rows, fold_map, margin_cells)


def extend_full(fields, fold_map, margin_cells):
    widened = with_halo(fields, (("lat", 1), ("lon", 2)), margin_cells)
    fold_rows = lax.all_gather(
        fields[:, fields.shape[1] - margin_cells :, :], "lon", axis=2, tiled=True
    )
    return place_fold(widened, fold_rows, fold_map, margin_cells)


def apply_power(source, source_depth, inverse_root, link_weights):
    outer_cut = STEPS - source_depth
    weighted = source * trim_margin(inverse_root, outer_cut)
    row_total = source.shape[-2] - 2
    column_total = source.shape[-1] - 2
    inner_weights = trim_margin(link_weights, outer_cut + 1)
    running = jnp.zeros((source.shape[0], row_total, column_total), jnp.float32)
    for direction_index in range(8):
        north_step, east_step = DIRECTIONS[direction_index]
        running = (
            running
            + inner_weights[direction_index]
            * weighted[
                :,
                1 + north_step : 1 + north_step + row_total,
                1 + east_step : 1 + east_step + column_total,
            ]
        )
    return -trim_margin(inverse_root, outer_cut + 1) * running


def advance(
    earlier, earlier_depth, current, current_depth, powers, stored, inverse_root, link_weights
):
    for power in powers:
        if power == STEPS - 1:
            earlier = earlier[:1]
            current = current[:1]
        upcoming = 2.0 * apply_power(
            current, current_depth, inverse_root, link_weights
        ) - trim_margin(earlier, earlier_depth - current_depth + 1)
        earlier, earlier_depth = (current, current_depth)
        current, current_depth = (upcoming, current_depth - 1)
        stored.append(trim_margin(current, current_depth))
    return (earlier, earlier_depth, current, current_depth)


def per_device(forcing, search_direction, ocean_depth, land_mask, fold_map):
    ocean_flag = land_mask.astype(jnp.float32)
    column_depth = ocean_depth * ocean_flag
    depth_wide = extend_depth(column_depth[None], fold_map, STEPS + 1)[0]
    wet_wide = (depth_wide > 0.0).astype(jnp.float32)
    centre_depth = trim_margin(depth_wide, 1)
    centre_wet = trim_margin(wet_wide, 1)
    row_total = depth_wide.shape[0] - 2
    column_total = depth_wide.shape[1] - 2
    weight_list = []
    link_sum = jnp.zeros_like(centre_depth)
    for direction_index in range(8):
        north_step, east_step = DIRECTIONS[direction_index]
        beside_depth = depth_wide[
            1 + north_step : 1 + north_step + row_total,
            1 + east_step : 1 + east_step + column_total,
        ]
        beside_wet = wet_wide[
            1 + north_step : 1 + north_step + row_total,
            1 + east_step : 1 + east_step + column_total,
        ]
        weight = (
            LINK_FACTORS[direction_index]
            * 0.5
            * (centre_depth + beside_depth)
            * centre_wet
            * beside_wet
        )
        weight_list.append(weight)
        link_sum = link_sum + weight
    link_weights = jnp.stack(weight_list)
    diagonal = centre_wet * (centre_depth / (REACH * REACH) + link_sum) + (1.0 - centre_wet)
    inverse_root = lax.rsqrt(diagonal)
    scaled_height = jnp.zeros_like(forcing)
    residual = ocean_flag * forcing
    direction = ocean_flag * search_direction
    chains = jnp.stack([direction, residual])
    earlier = extend_full(chains, fold_map, STEPS)
    earlier_depth = STEPS
    current = apply_power(earlier, earlier_depth, inverse_root, link_weights)
    current_depth = earlier_depth - 1
    stored = [trim_margin(earlier, earlier_depth), trim_margin(current, current_depth)]
    advance(
        earlier,
        earlier_depth,
        current,
        current_depth,
        range(1, STEPS),
        stored,
        inverse_root,
        link_weights,
    )
    krylov_basis = jnp.stack(
        [member[0] for member in stored] + [member[1] for member in stored[:STEPS]]
    )
    flattened = krylov_basis.reshape(krylov_basis.shape[0], -1)
    partial_gram = jnp.dot(flattened, flattened.T, precision=PRECISE)
    gram_matrix = lax.psum(partial_gram, ("lat", "lon"))
    solution_coords, residual_coords, direction_coords = coordinates(gram_matrix, STEPS)
    scaled_height = scaled_height + jnp.einsum(
        "k,kij->ij", solution_coords, krylov_basis, precision=PRECISE
    )
    residual = jnp.einsum("k,kij->ij", residual_coords, krylov_basis, precision=PRECISE)
    return (scaled_height, residual)


def solution(mesh):
    in_specs = (P("lat", "lon"), P("lat", "lon"), P("lat", "lon"), P("lat", "lon"), P())
    out_specs = (P("lat", "lon"), P("lat", "lon"))
    return jax.shard_map(
        per_device, mesh=mesh, in_specs=in_specs, out_specs=out_specs, check_vma=False
    )
```

profile of v0, /device:TPU:14, one launch (start us, length us, event | category | flops | bytes accessed | tf_op | source)
XLA Modules:
  0.0 225.7 jit_solution(7884336896558490846)
XLA Ops:
  0.7 1.0 copy.157
  1.7 1.0 copy.158
  2.6 1.0 copy.160
  3.6 1.0 copy.161
  4.7 0.7 fusion.205
  5.4 1.7 collective-permute-start.1
  7.6 1.0 fusion.110
  8.6 1.7 collective-permute-start.5
  10.4 0.6 fusion.120
  11.1 1.2 gather_fusion
  13.4 28.1 %all_gather.7 = f32[2,8,1024]{2,1,0:T(8,128)S(1)} all-gather(f32[2,8,128]{2,1,0:T(8,128)S(1)} %copy.165), channel_id=1, replica_groups=mesh['lat'=4,'lon'=8] {'lon'}, dimensions={2}, use_global_device_ids=true | all-gather | bytes 73728 | tf_op jit(solution)/shard_map/all_gather | solution.py:113
  41.5 1.2 gather_fusion.2
  43.2 0.6 pad_clamp_fusion
  43.8 0.7 fusion.123
  44.5 31.5 %all_gather.6 = f32[1,9,1024]{1,2,0:T(8,128)S(1)} all-gather(f32[1,9,128]{1,2,0:T(8,128)} %get-tuple-element.75), channel_id=1, replica_groups=mesh['lat'=4,'lon'=8] {'lon'}, dimensions={2}, use_global_device_ids=true | all-gather | bytes 41472 | tf_op jit(solution)/shard_map/all_gather | solution.py:105
  76.0 0.7 rev.6
  77.3 2.3 %rev.7 = f32[2,8,1024]{1,0,2:T(2,128)S(1)} reverse(f32[2,8,1024]{1,0,2:T(2,128)S(1)} %copy.166), dimensions={1} | reverse | bytes 131072 | tf_op jit(solution)/shard_map/rev | solution.py:92
  79.6 0.8 gather_fusion.1
  80.4 0.9 gather_fusion.3
  81.5 2.0 collective-permute-start.3
  83.7 1.9 collective-permute-start.6
  85.6 1.2 collective-permute-start.7
  87.3 0.7 slice_select_fusion.3
  96.3 0.7 pad_maximum_fusion
  98.4 2.9 %broadcast_multiply_fusion.1 = (f32[2,174,142]{1,0,2:T(2,128)S(1)}, f32[2,174,142]{1,0,2:T(2,128)S(1)}) fusion(f32[174,142]{0,1:T(8,128)S(1)} %get-tuple-element.65, f32[2,176,144]{1,0,2:T(2,128)S(1)} %get-tuple-element.14, f32[174,142]{0,1:T(8,128)S(1)} %get-tuple-element.77, f32[174,142]{0,1:T(8,128)S(1)} %get-tuple-element.84, ...), kind=kLoop, calls=%fused_computation.244 | loop fusion | flops 840072 | bytes 2964960 | tf_op jit(solution)/shard_map/mul | solution.py:121
  101.3 1.2 fusion.197
  102.5 2.6 %broadcast_multiply_fusion.2 = (f32[2,172,140]{1,0,2:T(2,128)S(1)}, f32[2,172,140]{1,0,2:T(2,128)S(1)}) fusion(f32[172,140]{0,1:T(8,128)S(1)} %get-tuple-element.63, f32[2,176,144]{1,0,2:T(2,128)S(1)} %get-tuple-element.15, f32[2,174,142]{1,0,2:T(2,128)S(1)} %get-tuple-element.12, f32[172,140]{0,1:T(8,128)S(1)} %get-tuple-element.85, ...), kind=kLoop, calls=%fused_computation.245 | loop fusion | flops 915040 | bytes 3082240 | tf_op jit(solution)/shard_map/mul | solution.py:121
  105.2 2.6 %broadcast_multiply_fusion.3 = (f32[2,170,138]{1,0,2:T(2,128)S(1)}, f32[2,170,138]{1,0,2:T(2,128)S(1)}) fusion(f32[170,138]{0,1:T(8,128)S(1)} %get-tuple-element.61, f32[2,174,142]{1,0,2:T(2,128)S(1)} %get-tuple-element.13, f32[2,172,140]{1,0,2:T(2,128)S(1)} %get-tuple-element.10, f32[170,138]{0,1:T(8,128)S(1)} %get-tuple-element.93, ...), kind=kLoop, calls=%fused_computation.246 | loop fusion | flops 891480 | bytes 3002880 | tf_op jit(solution)/shard_map/mul | solution.py:121
  107.8 1.3 fusion.199
  109.1 1.3 fusion.198
  110.4 2.5 %broadcast_multiply_fusion.4 = (f32[2,168,136]{1,0,2:T(2,128)S(1)}, f32[2,168,136]{1,0,2:T(2,128)S(1)}) fusion(f32[168,136]{0,1:T(8,128)S(1)} %get-tuple-element.59, f32[2,172,140]{1,0,2:T(2,128)S(1)} %get-tuple-element.11, f32[2,170,138]{1,0,2:T(2,128)S(1)} %get-tuple-element.8, f32[168,136]{0,1:T(8,128)S(1)} %get-tuple-element.101, ...), kind=kLoop, calls=%fused_computation.279 | loop fusion | flops 868224 | bytes 2924544 | tf_op jit(solution)/shard_map/mul | solution.py:121
  113.0 2.6 %broadcast_multiply_fusion.5 = (f32[2,166,134]{1,0,2:T(2,128)S(1)}, f32[2,166,134]{1,0,2:T(2,128)S(1)}) fusion(f32[166,134]{0,1:T(8,128)S(1)} %get-tuple-element.57, f32[2,170,138]{1,0,2:T(2,128)S(1)} %get-tuple-element.9, f32[2,168,136]{1,0,2:T(2,128)S(1)} %get-tuple-element.6, f32[166,134]{0,1:T(8,128)S(1)} %get-tuple-element.109, ...), kind=kLoop, calls=%fused_computation.280 | loop fusion | flops 845272 | bytes 2847232 | tf_op jit(solution)/shard_map/mul | solution.py:121
  115.6 1.3 fusion.201
  116.9 1.3 fusion.200
  118.2 2.5 %broadcast_multiply_fusion.6 = (f32[2,164,132]{1,0,2:T(2,128)S(1)}, f32[2,164,132]{1,0,2:T(2,128)S(1)}) fusion(f32[164,132]{0,1:T(8,128)S(1)} %get-tuple-element.55, f32[2,168,136]{1,0,2:T(2,128)S(1)} %get-tuple-element.7, f32[2,166,134]{1,0,2:T(2,128)S(1)} %get-tuple-element.4, f32[164,132]{0,1:T(8,128)S(1)} %get-tuple-element.117, ...), kind=kLoop, calls=%fused_computation.281 | loop fusion | flops 822624 | bytes 2770944 | tf_op jit(solution)/shard_map/mul | solution.py:121
  120.7 2.6 %slice_subtract_fusion.5 = f32[2,162,130]{1,0,2:T(2,128)S(1)} fusion(f32[2,166,134]{1,0,2:T(2,128)S(1)} %get-tuple-element.5, f32[2,164,132]{1,0,2:T(2,128)S(1)} %get-tuple-element.2, f32[162,130]{0,1:T(8,128)S(1)} %get-tuple-element.125, f32[162,130]{0,1:T(8,128)S(1)} %get-tuple-element.132, f32[162,130]{0,1:T(8,128)S(1)} %get-tuple-element.126, ...), kind=kLoop, calls=%fused_computation.161 | loop fusion | flops 758160 | bytes 2442960 | tf_op jit(solution)/shard_map/sub | solution.py:147
  123.3 1.3 fusion.203
  124.8 1.2 fusion.204
  126.3 1.9 fusion.202
  128.2 7.4 %stack.48 = f32[17,160,128]{1,0,2:T(8,128)S(1)} concatenate(f32[1,160,128]{1,0,2:T(1,128)S(1)} %copy.178, f32[1,160,128]{1,0,2:T(1,128)} %get-tuple-element.32, f32[1,160,128]{1,0,2:T(1,128)} %get-tuple-element.34, f32[1,160,128]{1,0,2:T(1,128)} %get-tuple-element.36, f32[1,160,128]{1,0,2:T(1,128)} %get-tuple-element.38, f32[1,160,128]{1,0,2:T(1,128)} %get-tuple-element.40, ...), dimensions={0} | concatenate | bytes 2785280 | tf_op jit(solution)/shard_map/stack | solution.py:208
  135.6 3.4 %convolution_bitcast_fusion = f32[17,17]{1,0:T(8,128)S(1)} fusion(f32[17,160,128]{1,0,2:T(8,128)S(1)} %stack.48), kind=kOutput, calls=%fused_computation.4 | convolution fusion | flops 71024640 | bytes 1393796 | tf_op jit(solution)/shard_map/dot_general | solution.py:212
  139.0 46.3 %psum.7 = f32[17,17]{1,0:T(8,128)S(1)} all-reduce(f32[17,17]{1,0:T(8,128)S(1)} %convolution_bitcast_fusion), channel_id=1, replica_groups=mesh['lat'=4,'lon'=8] {'lat','lon'}, use_global_device_ids=true, to_apply=%region_0.1 | all-reduce | flops 289 | bytes 2312 | tf_op jit(solution)/shard_map/psum | solution.py:213
  185.3 0.7 fusion.17
  186.0 0.7 fusion.16
  188.1 0.7 fusion.130
  188.8 0.7 fusion.18
  190.9 0.7 bitcast_add_fusion
  191.7 0.8 fusion.19
  193.8 0.7 fusion.20
  196.0 0.8 fusion.21
  198.2 0.7 fusion.22
  200.4 0.8 fusion.23
  202.5 0.7 fusion.24
  204.7 0.8 fusion.25
  206.8 0.7 fusion.26
  209.0 0.8 fusion.27
  211.1 0.7 fusion.28
  213.4 0.8 fusion.29
  215.5 0.7 fusion.30
  217.7 0.8 fusion.31
  219.8 1.7 fusion.131
  221.5 2.4 %fusion.133 = f32[1,160,128]{1,0,2:T(1,128)S(1)} fusion(f32[17,160,128]{1,0,2:T(8,128)S(1)} %stack.48, f32[17]{0:T(128)S(1)} %multiply_add_fusion, f32[17]{0:T(128)S(1)} %multiply_add_fusion.1, f32[17]{0:T(128)S(1)} %multiply_add_fusion.2, f32[17]{0:T(128)S(1)} %multiply_add_fusion.3, f32[17]{0:T(128)S(1)} %multiply_add_fusion.4, ...), kind=kOutput, calls=%fused_computation.364 | convolution fusion | flops 4178175 | bytes 1475580 | tf_op jit(solution)/shard_map/k,kij->ij/dot_general | solution.py:215
  224.0 0.7 copy.217
  224.7 0.7 copy.216
  (119 shorter events, 14.2 us)
Async XLA Ops:
  0.6 10.4 %copy-start = (s32[1024]{0:T(1024)S(1)}, s32[1024]{0:T(1024)}, u32[]{:S(2)}) copy-start(s32[1024]{0:T(1024)} %param.10) | copy-start | bytes 12292
  0.6 43.2 %copy-start.1 = (f32[17,17]{1,0:T(8,128)S(1)}, f32[17,17]{1,0:T(8,128)}, u32[]{:S(2)}) copy-start(f32[17,17]{1,0:T(8,128)} %constant.118.clone) | copy-start | bytes 3472
  5.4 76.0 %collective-permute-start = (f32[1,9,128]{1,2,0:T(8,128)}, f32[1,9,128]{1,2,0:T(8,128)S(1)}, u32[]{:S(2)}, u32[]{:S(2)}) collective-permute-start(f32[1,9,128]{1,2,0:T(8,128)} %get-tuple-element.75), channel_id=1, source_target_pairs={{0,8},{8,16},{16,24},{24,0},{1,9},{9,17},{17,25},{25,1},{2,10},{10... | collective-permute-start | bytes 13832 | tf_op jit(solution)/shard_map/ppermute | solution.py:23
  5.4 76.0 %collective-permute-start.1 = (f32[1,9,128]{1,2,0:T(8,128)}, f32[1,9,128]{1,2,0:T(8,128)S(1)}, u32[]{:S(2)}, u32[]{:S(2)}) collective-permute-start(f32[1,9,128]{1,2,0:T(8,128)} %get-tuple-element.76), channel_id=1, source_target_pairs={{8,0},{16,8},{24,16},{0,24},{9,1},{17,9},{25,17},{1,25},{10,2},{18... | collective-permute-start | bytes 13832 | tf_op jit(solution)/shard_map/ppermute | solution.py:24
  8.6 74.9 %collective-permute-start.4 = (f32[2,8,128]{1,0,2:T(2,128)S(1)}, f32[2,8,128]{1,0,2:T(2,128)S(1)}, u32[]{:S(2)}, u32[]{:S(2)}) collective-permute-start(f32[2,8,128]{1,0,2:T(2,128)S(1)} %get-tuple-element.46), channel_id=1, source_target_pairs={{0,8},{8,16},{16,24},{24,0},{1,9},{9,17},{17,25},{25,1},{2,10},{10... | collective-permute-start | bytes 24584 | tf_op jit(solution)/shard_map/ppermute | solution.py:23
  8.6 74.9 %collective-permute-start.5 = (f32[2,8,128]{1,0,2:T(2,128)}, f32[2,8,128]{1,0,2:T(2,128)S(1)}, u32[]{:S(2)}, u32[]{:S(2)}) collective-permute-start(f32[2,8,128]{1,0,2:T(2,128)} %get-tuple-element.47), channel_id=1, source_target_pairs={{8,0},{16,8},{24,16},{0,24},{9,1},{17,9},{25,17},{1,25},{10,2},{18... | collective-permute-start | bytes 24584 | tf_op jit(solution)/shard_map/ppermute | solution.py:24
  10.4 34.1 %copy-start.4 = (pred[17,17]{1,0:T(8,128)(4,1)}, pred[17,17]{1,0:T(8,128)(4,1)S(1)}, u32[]{:S(2)}) copy-start(pred[17,17]{1,0:T(8,128)(4,1)S(1)} %iota_compare_fusion) | copy-start | bytes 871
  81.4 5.4 %collective-permute-start.2 = (f32[1,178,9]{1,2,0:T(8,128)S(1)}, f32[1,178,9]{1,2,0:T(8,128)S(1)}, u32[]{:S(2)}, u32[]{:S(2)}) collective-permute-start(f32[1,178,9]{1,2,0:T(8,128)S(1)} %get-tuple-element.48), channel_id=1, source_target_pairs={{0,1},{1,2},{2,3},{3,4},{4,5},{5,6},{6,7},{7,0},{8,9},{9,10},{10,1... | collective-permute-start | bytes 19232 | tf_op jit(solution)/shard_map/ppermute | solution.py:23
  81.5 5.6 %collective-permute-start.3 = (f32[1,178,9]{1,2,0:T(8,128)S(1)}, f32[1,178,9]{1,2,0:T(8,128)S(1)}, u32[]{:S(2)}, u32[]{:S(2)}) collective-permute-start(f32[1,178,9]{1,2,0:T(8,128)S(1)} %get-tuple-element.49), channel_id=1, source_target_pairs={{1,0},{2,1},{3,2},{4,3},{5,4},{6,5},{7,6},{0,7},{9,8},{10,9},{11,1... | collective-permute-start | bytes 19232 | tf_op jit(solution)/shard_map/ppermute | solution.py:24
  83.5 5.2 %copy-start.2 = (f32[2,8,128]{1,0,2:T(2,128)}, f32[2,8,128]{1,0,2:T(2,128)S(1)}, u32[]{:S(2)}) copy-start(f32[2,8,128]{1,0,2:T(2,128)S(1)} %collective-permute-done.5) | copy-start | bytes 24580
  83.7 12.6 %collective-permute-start.6 = (f32[2,176,8]{1,0,2:T(2,128)S(1)}, f32[2,176,8]{1,0,2:T(2,128)S(1)}, u32[]{:S(2)}, u32[]{:S(2)}) collective-permute-start(f32[2,176,8]{1,0,2:T(2,128)S(1)} %get-tuple-element.27), channel_id=1, source_target_pairs={{0,1},{1,2},{2,3},{3,4},{4,5},{5,6},{6,7},{7,0},{8,9},{9,10},{10,1... | collective-permute-start | bytes 33800 | tf_op jit(solution)/shard_map/ppermute | solution.py:23
  85.6 10.6 %collective-permute-start.7 = (f32[2,176,8]{1,0,2:T(2,128)S(1)}, f32[2,176,8]{1,0,2:T(2,128)S(1)}, u32[]{:S(2)}, u32[]{:S(2)}) collective-permute-start(f32[2,176,8]{1,0,2:T(2,128)S(1)} %get-tuple-element.28), channel_id=1, source_target_pairs={{1,0},{2,1},{3,2},{4,3},{5,4},{6,5},{7,6},{0,7},{9,8},{10,9},{11,1... | collective-permute-start | bytes 33800 | tf_op jit(solution)/shard_map/ppermute | solution.py:24
  94.9 1.4 copy-start.3
  95.2 2.2 copy-start.7
  135.6 49.7 %copy-start.5 = (pred[17,17]{1,0:T(8,128)(4,1)S(1)}, pred[17,17]{1,0:T(8,128)(4,1)}, u32[]{:S(2)}) copy-start(pred[17,17]{1,0:T(8,128)(4,1)} %copy-done.4) | copy-start | bytes 871
  135.6 50.4 %copy-start.6 = (f32[1,17]{1,0:T(1,128)S(1)}, f32[1,17]{1,0:T(1,128)}, u32[]{:S(2)}) copy-start(f32[1,17]{1,0:T(1,128)} %fusion.123) | copy-start | bytes 208
where the time goes:
time: 230 us; the launch traced here: 226 us
  blocking collectives  106 us (46%)
  local copies, waits for them, and re-layouts  37.6 us (16%)
  other arithmetic  30.4 us (13%)
  between operations  21.8 us (9%)
  matrix products  21.1 us (9%)
  starting transfers between devices  8.72 us (4%)
    psum x1, blocking collectives, per_device(): gram_matrix = lax.psum(partial_gram, ('lat', 'lon'))  46.3 us
    all_gather x1, blocking collectives, extend_depth(): lax.all_gather(fields[:, fields.shape[1] - margin_cells:, :], 'lon', axis...  31.5 us
    all_gather x1, blocking collectives, extend_full(): lax.all_gather(fields[:, fields.shape[1] - margin_cells:, :], 'lon', axis...  28.1 us
    mul x8, other arithmetic, apply_power(): weighted = source * trim_margin(inverse_root, outer_cut)  16.5 us
    slice x6, local copies, waits for them, and re-layouts, per_device(): member[1]  7.88 us
    another operation x1, local copies, waits for them, and re-layouts, per_device(): jnp.stack([member[0] for member in stored] + [member[1] for member in sto...  7.44 us
    ppermute x4, starting transfers between devices, with_halo(): after = lax.ppermute(leading, axis, down)  6.73 us
    dot_general x8, matrix products, coordinates(): jnp.dot(gram_matrix, mapped, precision=PRECISE)  6.05 us
  transfers between devices with their start and end apart: 8, of which 1 were waited for; matrix products, arithmetic and copies ran while one was open for 10% of the time, Pallas kernels for 0%

commit v1 on v0

v1 whole, which is shorter than its diff:
```python
import functools

import jax
import jax.numpy as jnp
from jax import lax
from jax.experimental import pallas as pl
from jax.experimental.pallas import tpu as pltpu
from jax.sharding import PartitionSpec as P

STEPS = 8
REACH = 256
MESH = pl.DeviceIdType.MESH
PAD = 16
GROUP = 32
CHUNK = 16

DIRECTIONS = ((1, 0), (-1, 0), (0, 1), (0, -1), (1, 1), (-1, -1), (1, -1), (-1, 1))
SLOT = {offset: index for index, offset in enumerate(DIRECTIONS)}


def halves(offset):
    return 0.5 if 0 in offset else 0.25


def chunks_of(low, high, size):
    return [(at, min(size, high - at)) for at in range(low, high, size)]


def shift_pair(centre, halo, step):
    width = centre.shape[1]
    lane = lax.broadcasted_iota(jnp.int32, centre.shape, 1)
    edge = lane == (0 if step == 1 else width - 1)
    turn = width - 1 if step == 1 else 1
    return (
        pltpu.roll(jnp.where(edge, halo, centre), turn, 1),
        pltpu.roll(jnp.where(edge, centre, halo), turn, 1),
    )


def turned(x, shift):
    shift = shift % x.shape[1]
    return x if shift == 0 else pltpu.roll(x, shift, 1)


def bilinear(left, right, gram):
    total = None
    for i in sorted(left):
        inner = None
        for j in sorted(right):
            term = gram(i, j) * right[j]
            inner = term if inner is None else inner + term
        inner = left[i] * inner
        total = inner if total is None else total + inner
    return total


def plus(left, right):
    result = dict(left)
    for key, value in right.items():
        result[key] = result[key] + value if key in result else value
    return result


def scaled(factor, vector):
    return {key: factor * value for key, value in vector.items()}


def apply_shift(vector):
    result = {}
    for (chain, power), value in vector.items():
        parts = [((chain, power), value)]
        if power == 0:
            parts.append(((chain, 1), value))
        else:
            half = 0.5 * value
            parts += [((chain, power + 1), half), ((chain, power - 1), half)]
        result = plus(result, {}) if not parts else result
        for key, part in parts:
            result = plus(result, {key: part})
    return result


def coordinates(moments):
    cache = {}

    def gram(left, right):
        kind = (left[0], right[0]) if left[0] <= right[0] else (right[0], left[0])
        low, high = sorted((left[1], right[1]))
        key = (kind, low, high)
        if key not in cache:
            series = moments[kind]
            cache[key] = 0.5 * (series[high + low] + series[high - low])
        return cache[key]

    solution_coords = {}
    one = jnp.ones_like(moments[("p", "p")][0])
    direction_coords = {("p", 0): one}
    residual_coords = {("r", 0): one}
    norm_now = bilinear(residual_coords, residual_coords, gram)
    for _ in range(STEPS):
        mapped = apply_shift(direction_coords)
        step_length = norm_now / bilinear(direction_coords, mapped, gram)
        solution_coords = plus(solution_coords, scaled(step_length, direction_coords))
        residual_coords = plus(residual_coords, scaled(-step_length, mapped))
        norm_next = bilinear(residual_coords, residual_coords, gram)
        direction_coords = plus(
            residual_coords, scaled(norm_next / norm_now, direction_coords)
        )
        norm_now = norm_next
    return solution_coords, residual_coords


def fold_sublanes(parts):
    row = lax.broadcasted_iota(jnp.int32, parts[0].shape, 0)
    parts = list(parts)
    span = 4
    while span:
        low = (row & span) == 0
        half = len(parts) // 2
        parts = [
            jnp.where(low, first, second)
            + pltpu.roll(jnp.where(low, second, first), span, 0)
            if span == 4
            else jnp.where(low, first, second)
            + jnp.where(low, pltpu.roll(first, 8 - span, 0), pltpu.roll(second, span, 0))
            for first, second in zip(parts[:half], parts[half:])
        ]
        span //= 2
    return parts[0]


def kernel(
    n_lat, n_lon, forcing, search, depth_in, mask_in, fold_map, out_height, out_residual,
    depth, depth_e, depth_w, root, root_e, root_w, weights, basis, basis_halo,
    row_north, row_south, fold_rows, packed, got_north, got_south, got_east, got_west,
    corners, fold_all, dots, sums_lat, sums_lon, moment_rows,
    near_send, near_recv, fold_send, fold_recv, lat_send, lat_recv, lon_send, lon_recv,
):
    rows, width = forcing.shape
    lat, lon = lax.axis_index("lat"), lax.axis_index("lon")
    top = n_lat - 1
    north, south = lax.rem(lat + 1, n_lat), lax.rem(lat + n_lat - 1, n_lat)
    east, west = lax.rem(lon + 1, n_lon), lax.rem(lon + n_lon - 1, n_lon)
    has_north, has_south = lat < top, lat > 0
    group_rows = rows * GROUP // width
    n_groups = width // GROUP

    barrier = pltpu.get_barrier_semaphore()

    def greet(place):
        pl.semaphore_signal(barrier, inc=1, device_id=place, device_id_type=MESH)

    for d in range(1, n_lat):
        greet((lax.rem(lat + d, n_lat), lon))
    for d in range(1, n_lon):
        greet((lat, lax.rem(lon + d, n_lon)))

    for place in ((north, east), (north, west), (south, east), (south, west)):
        greet(place)

    lane_group = lax.broadcasted_iota(jnp.int32, (group_rows, width), 1)
    west_edge = east_edge = None
    for g in range(n_groups):
        here = pl.ds(g * group_rows, group_rows)
        there = pl.ds(PAD + g * group_rows, group_rows)
        flag = mask_in[here, :].astype(jnp.float32)
        deep = depth_in[here, :] * flag
        moving = search[here, :] * flag
        left = forcing[here, :] * flag
        depth[0, there, :] = deep
        basis[0, there, :] = moving
        basis[STEPS + 1, there, :] = left
        inside = lane_group - g * GROUP
        to_west = jnp.where(
            inside < 9,
            turned(deep, g * GROUP),
            jnp.where(inside < 17, turned(moving, g * GROUP + 9), turned(left, g * GROUP + 17)),
        )
        to_east = jnp.where(
            inside < 9,
            turned(deep, g * GROUP + 9),
            jnp.where(inside < 17, turned(moving, g * GROUP + 17), turned(left, g * GROUP + 25)),
        )
        west_edge = to_west if g == 0 else jnp.where(inside >= 0, to_west, west_edge)
        east_edge = to_east if g == 0 else jnp.where(inside >= 0, to_east, east_edge)
    packed[0] = west_edge
    packed[1] = east_edge
    first, last = PAD, PAD + rows
    row_south[0:16, :] = depth[0, first : first + 16, :]
    row_south[16:24, :] = basis[0, first : first + 8, :]
    row_south[24:32, :] = basis[STEPS + 1, first : first + 8, :]
    row_north[0:16, :] = depth[0, last - 16 : last, :]
    row_north[16:24, :] = basis[0, last - 8 : last, :]
    row_north[24:32, :] = basis[STEPS + 1, last - 8 : last, :]

    @pl.when(lat == top)
    def _():
        for r in range(16):
            fold_rows[r : r + 1, :] = depth[0, last - 1 - r : last - r, :]
        for r in range(8):
            fold_rows[16 + r : 17 + r, :] = basis[0, last - 1 - r : last - r, :]
            fold_rows[24 + r : 25 + r, :] = basis[STEPS + 1, last - 1 - r : last - r, :]
        fold_all[lon] = fold_rows[...]

    pl.semaphore_wait(barrier, n_lat - 1 + n_lon - 1 + 4)

    def near(index, source, target, place):
        return pltpu.make_async_remote_copy(
            src_ref=source, dst_ref=target, send_sem=near_send.at[index],
            recv_sem=near_recv.at[index], device_id=place, device_id_type=MESH,
        )

    tail = pl.ds(group_rows - 16, 16)
    head = pl.ds(0, 16)
    to_north = near(0, row_north, got_south, (north, lon))
    to_south = near(1, row_south, got_north, (south, lon))
    to_east = near(2, packed.at[1], got_west, (lat, east))
    to_west = near(3, packed.at[0], got_east, (lat, west))
    to_ne = near(4, packed.at[1, tail], corners.at[0], (north, east))
    to_nw = near(5, packed.at[0, tail], corners.at[1], (north, west))
    to_se = near(6, packed.at[1, head], corners.at[2], (south, east))
    to_sw = near(7, packed.at[0, head], corners.at[3], (south, west))
    northward, southward = (to_north, to_ne, to_nw), (to_south, to_se, to_sw)

    def spread(source, slots, send_sem, recv_sem, along_lat):
        size = n_lat if along_lat else n_lon
        me = lat if along_lat else lon
        copies = []
        for d in range(1, size):
            peer = lax.rem(me + d, size)
            copies.append(
                pltpu.make_async_remote_copy(
                    src_ref=source, dst_ref=slots.at[me], send_sem=send_sem.at[d - 1],
                    recv_sem=recv_sem.at[d - 1],
                    device_id=(peer, lon) if along_lat else (lat, peer),
                    device_id_type=MESH,
                )
            )
        return copies

    across = spread(fold_rows, fold_all, fold_send, fold_recv, False)

    @pl.when(lat == top)
    def _():
        for copy in across:
            copy.start()

    to_east.start()
    to_west.start()

    @pl.when(has_north)
    def _():
        for copy in northward:
            copy.start()

    @pl.when(has_south)
    def _():
        for copy in southward:
            copy.start()

    def unpack(got_e, got_w, start, g, count):
        lane = lax.broadcasted_iota(jnp.int32, (count, width), 1)
        base = -g * GROUP
        spans = ((0, 9, depth.at[1]), (9, 8, basis_halo.at[0]), (17, 8, basis_halo.at[STEPS + 1]))
        for offset, cells, target in spans:
            from_east = turned(got_e, base - offset)
            from_west = turned(got_w, base - offset - cells)
            target[start : start + count, :] = jnp.where(
                lane < cells,
                from_east,
                jnp.where(lane >= width - cells, from_west, jnp.zeros_like(got_e)),
            )

    to_east.wait_recv()
    to_west.wait_recv()
    for g in range(n_groups):
        unpack(got_east[...], got_west[...], PAD + g * group_rows, g, group_rows)

    @pl.when(has_south)
    def _():
        for copy in northward:
            copy.wait_recv()
        depth[0, 0:16, :] = got_south[0:16, :]
        basis[0, 8:16, :] = got_south[16:24, :]
        basis[STEPS + 1, 8:16, :] = got_south[24:32, :]
        unpack(corners[1], corners[0], 0, n_groups - 1, 16)

    @pl.when(lat == 0)
    def _():
        nothing = jnp.zeros((16, width), jnp.float32)
        for target in (depth.at[0], depth.at[1]):
            target[0:16, :] = nothing
        for power in (0, STEPS + 1):
            basis[power, 0:16, :] = nothing
            basis_halo[power, 0:16, :] = nothing

    @pl.when(has_north)
    def _():
        for copy in southward:
            copy.wait_recv()
        depth[0, last : last + 16, :] = got_north[0:16, :]
        basis[0, last : last + 8, :] = got_north[16:24, :]
        basis[STEPS + 1, last : last + 8, :] = got_north[24:32, :]
        unpack(corners[3], corners[2], last, 0, 16)

    @pl.when(lat == top)
    def _():
        for copy in across:
            copy.wait_recv()
        total = n_lon * width
        pivot = lax.rem(fold_map[0] - lon * width + total, total)
        block, offset = pivot // width, lax.rem(pivot, width)
        lane = lax.broadcasted_iota(jnp.int32, (32, width), 1)
        index = lax.rem(offset - lane + width, width)

        def mirrored(which):
            rows_of = fold_all[lax.rem(block + which + n_lon, n_lon)]
            return jnp.take_along_axis(rows_of, index, axis=1, mode="promise_in_bounds")

        ahead, same, behind, beyond = (mirrored(which) for which in (1, 0, -1, -2))
        close = lane <= offset
        centre = jnp.where(close, same, behind)
        halo = jnp.where(
            lane < width // 2, jnp.where(close, behind, beyond), jnp.where(close, ahead, same)
        )
        for value, deep, fields in ((centre, depth.at[0], basis), (halo, depth.at[1], basis_halo)):
            deep[last : last + 16, :] = value[0:16, :]
            fields[0, last : last + 8, :] = value[16:24, :]
            fields[STEPS + 1, last : last + 8, :] = value[24:32, :]

    low, high = PAD - 8, last + 8
    for at, count in chunks_of(0, rows + 2 * PAD, CHUNK):
        span = pl.ds(at, count)
        centre, halo = depth[0, span, :], depth[1, span, :]
        depth_e[0, span, :], depth_e[1, span, :] = shift_pair(centre, halo, 1)
        depth_w[0, span, :], depth_w[1, span, :] = shift_pair(centre, halo, -1)
    shifted_depth = {0: depth, 1: depth_e, -1: depth_w}
    for at, count in chunks_of(low, high, CHUNK):
        roots = []
        for tile in (0, 1):
            here = depth[tile, at : at + count, :]
            sums = {0.5: None, 0.25: None}
            for a, b in DIRECTIONS:
                beside = shifted_depth[b][tile, at + a : at + a + count, :]
                link = jnp.where(beside > 0.0, here + beside, 0.0)
                factor = halves((a, b))
                sums[factor] = link if sums[factor] is None else sums[factor] + link
            diagonal = here * (1.0 / (REACH * REACH)) + (0.5 * sums[0.5] + 0.25 * sums[0.25])
            value = lax.rsqrt(jnp.where(here > 0.0, diagonal, 1.0))
            root[tile, at : at + count, :] = value
            roots.append(value)
        span = pl.ds(at, count)
        root_e[0, span, :], root_e[1, span, :] = shift_pair(roots[0], roots[1], 1)
        root_w[0, span, :], root_w[1, span, :] = shift_pair(roots[0], roots[1], -1)
    shifted_root = {0: root, 1: root_e, -1: root_w}
    for at, count in chunks_of(low, high, CHUNK):
        for tile in (0, 1):
            for b in (-1, 0, 1):
                goal_depth = shifted_depth[-b][tile, at : at + count, :]
                goal_root = shifted_root[-b][tile, at : at + count, :]
                goal_wet = goal_depth > 0.0
                for a in (-1, 0, 1):
                    if (a, b) == (0, 0):
                        continue
                    from_depth = depth[tile, at + a : at + a + count, :]
                    from_root = root[tile, at + a : at + a + count, :]
                    link = jnp.where(
                        jnp.minimum(goal_depth, from_depth) > 0.0, goal_depth + from_depth, 0.0
                    )
                    weights[SLOT[(a, b)], tile, at : at + count, :] = (
                        goal_root * (-2.0 * halves((a, b)))
                    ) * (link * from_root)

    dot_sums = {}

    def add_dot(key, left, right):
        product = left * right
        for r in range(0, product.shape[0], 8):
            piece = product[r : r + 8, :]
            dot_sums[key] = piece if key not in dot_sums else dot_sums[key] + piece

    row_chunks = [(low, 8)] + chunks_of(first, last, CHUNK) + [(last, 8)]
    for at, count in chunks_of(first, last, CHUNK):
        p0 = basis[0, at : at + count, :]
        r0 = basis[STEPS + 1, at : at + count, :]
        add_dot(("p", "p", 0), p0, p0)
        add_dot(("r", "r", 0), r0, r0)
        add_dot(("p", "r", 0), p0, r0)

    for power in range(1, STEPS + 1):
        chains = [("p", 0, power == STEPS)]
        if power < STEPS:
            chains.append(("r", STEPS + 1, power == STEPS - 1))
        for at, count in row_chunks:
            inner = first <= at < last
            fresh = {}
            held = {}
            factors = [
                {ab: weights[SLOT[ab], tile, at : at + count, :] for ab in DIRECTIONS}
                for tile in (0, 1)
            ]
            for name, origin, only_block in chains:
                if only_block and not inner:
                    continue
                slot = origin + power
                parts = []
                for tile, fields in ((0, basis), (1, basis_halo)):
                    taken = {
                        a: fields[slot - 1, at + a : at + a + count, :] for a in (-1, 0, 1)
                    }
                    if tile == 0:
                        held[name] = taken[0]
                    columns = {}
                    for b in (-1, 0, 1):
                        total = None
                        for a in (-1, 0, 1):
                            if (a, b) == (0, 0):
                                continue
                            term = factors[tile][(a, b)] * taken[a]
                            total = term if total is None else total + term
                        columns[b] = total
                    parts.append(columns)
                ahead = shift_pair(parts[0][1], parts[1][1], 1)
                behind = shift_pair(parts[0][-1], parts[1][-1], -1)
                for tile, fields in ((0, basis), (1, basis_halo)):
                    if tile == 1 and only_block:
                        continue
                    value = parts[tile][0] + ahead[tile] + behind[tile]
                    if power == 1:
                        value = 0.5 * value
                    else:
                        value = value - fields[slot - 2, at : at + count, :]
                    fields[slot, at : at + count, :] = value
                    if tile == 0:
                        fresh[name] = value
            if not inner:
                continue
            for name, _, _ in chains:
                add_dot((name, name, 2 * power), fresh[name], fresh[name])
                add_dot((name, name, 2 * power - 1), fresh[name], held[name])
            if power < STEPS:
                add_dot(("p", "r", 2 * power), fresh["p"], fresh["r"])
                add_dot(("p", "r", 2 * power - 1), fresh["p"], held["r"])
            else:
                add_dot(
                    ("p", "r", 2 * power - 1),
                    fresh["p"],
                    basis[STEPS + power, at : at + count, :],
                )
        for key in [key for key in dot_sums]:
            dots[order_of()[key]] = dot_sums.pop(key)

    number = len(order_of())
    lane = lax.broadcasted_iota(jnp.int32, (8, width), 1)
    message = jnp.zeros((8, width), jnp.float32)
    for g in range(number // 8):
        grouped = fold_sublanes([dots[8 * g + s] for s in range(8)])
        message = jnp.where(lane == g, jnp.sum(grouped, axis=1, keepdims=True), message)
    for slots, size, along_lat, send_sem, recv_sem in (
        (sums_lat, n_lat, True, lat_send, lat_recv),
        (sums_lon, n_lon, False, lon_send, lon_recv),
    ):
        me = lat if along_lat else lon
        slots[me] = message
        copies = spread(slots.at[me], slots, send_sem, recv_sem, along_lat)
        for copy in copies:
            copy.start()
        for copy in copies:
            copy.wait_recv()
        message = slots[0]
        for index in range(1, size):
            message = message + slots[index]
        for copy in copies:
            copy.wait_send()
    for g in range(number // 8):
        picked = jnp.sum(jnp.where(lane == g, message, 0.0), axis=1, keepdims=True)
        moment_rows[8 * g : 8 * g + 8, :] = jnp.broadcast_to(picked, (8, width))
    moments = {}
    for kind in (("p", "p"), ("p", "r"), ("r", "r")):
        series = []
        for index in range(17 if kind == ("p", "p") else 16 if kind == ("p", "r") else 15):
            spot = order_of()[kind + (index,)]
            value = jnp.broadcast_to(moment_rows[spot : spot + 1, :], (8, width))
            series.append(value if index < 2 else 2.0 * value - series[index % 2])
        moments[kind] = series
    height_coords, residual_coords = coordinates(moments)
    for at in range(0, rows, 8):
        for coords, out in ((height_coords, out_height), (residual_coords, out_residual)):
            total = None
            for (chain, power), factor in sorted(coords.items(), key=lambda item: item[0]):
                slot = power + (0 if chain == "p" else STEPS + 1)
                term = factor * basis[slot, PAD + at : PAD + at + 8, :]
                total = term if total is None else total + term
            out[at : at + 8, :] = total

    to_east.wait_send()
    to_west.wait_send()

    @pl.when(has_north)
    def _():
        for copy in northward:
            copy.wait_send()

    @pl.when(has_south)
    def _():
        for copy in southward:
            copy.wait_send()

    @pl.when(lat == top)
    def _():
        for copy in across:
            copy.wait_send()


@functools.cache
def order_of():
    keys = [("p", "p", k) for k in range(2 * STEPS + 1)]
    keys += [("p", "r", k) for k in range(2 * STEPS)]
    keys += [("r", "r", k) for k in range(2 * STEPS - 1)]
    return {key: index for index, key in enumerate(keys)}


def per_device(n_lat, n_lon, forcing, search_direction, ocean_depth, land_mask, fold_map):
    rows, width = forcing.shape
    tall = rows + 2 * PAD
    f32 = jnp.float32
    pair = pltpu.VMEM((2, tall, width), f32)
    edge = pltpu.VMEM((32, width), f32)
    group_rows = rows * GROUP // width
    strip = pltpu.VMEM((group_rows, width), f32)
    dma = pltpu.SemaphoreType.DMA
    block = pl.BlockSpec(memory_space=pltpu.VMEM)
    return pl.pallas_call(
        functools.partial(kernel, n_lat, n_lon),
        out_shape=[jax.ShapeDtypeStruct((rows, width), f32)] * 2,
        in_specs=[block] * 4 + [pl.BlockSpec(memory_space=pltpu.SMEM)],
        out_specs=[block] * 2,
        scratch_shapes=[
            pair, pair, pair, pair, pair, pair,
            pltpu.VMEM((8, 2, tall, width), f32),
            pltpu.VMEM((2 * STEPS + 1, tall, width), f32),
            pltpu.VMEM((2 * STEPS + 1, tall, width), f32),
            edge, edge, edge,
            pltpu.VMEM((2, group_rows, width), f32),
            edge, edge, strip, strip,
            pltpu.VMEM((4, 16, width), f32),
            pltpu.VMEM((n_lon, 32, width), f32),
            pltpu.VMEM((6 * STEPS, 8, width), f32),
            pltpu.VMEM((n_lat, 8, width), f32),
            pltpu.VMEM((n_lon, 8, width), f32),
            pltpu.VMEM((6 * STEPS, width), f32),
            dma((8,)), dma((8,)),
            dma((n_lon - 1,)), dma((n_lon - 1,)),
            dma((n_lat - 1,)), dma((n_lat - 1,)),
            dma((n_lon - 1,)), dma((n_lon - 1,)),
        ],
        compiler_params=pltpu.CompilerParams(collective_id=0, has_side_effects=True),
        name="tripole_cg",
    )(forcing, search_direction, ocean_depth, land_mask, fold_map)


def solution(mesh):
    cells = P("lat", "lon")
    return jax.shard_map(
        functools.partial(per_device, mesh.shape["lat"], mesh.shape["lon"]),
        mesh=mesh,
        in_specs=(cells, cells, cells, cells, P()),
        out_specs=(cells, cells),
        check_vma=False,
    )
```

time: 230 us -> 27.4 us (0.12)
  the two profiles are of different devices: /device:TPU:14 before, /device:TPU:0 now
where the time goes in v1:
time: 27.4 us; the launch traced here: 27.2 us
  Pallas kernels  24.3 us (89%)
  local copies, waits for them, and re-layouts  2.2 us (8%)
  between operations  0.65 us (2%)
    pallas_call x1, Pallas kernels, per_device(): pl.pallas_call(functools.partial(kernel, n_lat, n_lon), out_shape=[jax.Sh...  24.3 us
    unnamed x4, local copies, waits for them, and re-layouts  2.2 us

profile of v1, /device:TPU:0, one launch (start us, length us, event | category | flops | bytes accessed | tf_op | source)
XLA Modules:
  0.0 27.2 jit_solution(1501711554416194910)
XLA Ops:
  0.6 24.3 %tripole_cg.1 = (f32[160,128]{1,0:T(8,128)}, f32[160,128]{1,0:T(8,128)}) custom-call(f32[160,128]{1,0:T(8,128)} %forcing.1, f32[160,128]{1,0:T(8,128)} %search.1, f32[160,128]{1,0:T(8,128)} %depth_in.1, s32[160,128]{1,0:T(8,128)} %mask_in.1, s32[1024]{0:T(1024)} %fold_map.1), custom_call_target="tpu_custom_call" | custom-call | tf_op jit(solution)/shard_map/tripole_cg/pallas_call | solution.py:533
  24.9 0.0 copy-start
  25.0 1.6 %copy.9 = f32[160,128]{1,0:T(8,128)} copy(f32[160,128]{1,0:T(8,128)} %get-tuple-element.4) | data formatting | bytes 163840
  26.5 0.0 copy-done
  26.5 0.6 %copy.10 = f32[160,128]{1,0:T(8,128)} copy(f32[160,128]{1,0:T(8,128)S(1)} %copy-done) | data formatting | bytes 163840
Async XLA Ops:
  24.9 1.6 %copy-start = (f32[160,128]{1,0:T(8,128)S(1)}, f32[160,128]{1,0:T(8,128)}, u32[]{:S(2)}) copy-start(f32[160,128]{1,0:T(8,128)} %get-tuple-element.5) | copy-start | bytes 245764

commit v2 on v1

--- a/solution.py
+++ b/solution.py
@@ -13,6 +13,7 @@
 PAD = 16
 GROUP = 32
 CHUNK = 16
+DIRECT_LIMIT = 64
 
 DIRECTIONS = ((1, 0), (-1, 0), (0, 1), (0, -1), (1, 1), (-1, -1), (1, -1), (-1, 1))
 SLOT = {offset: index for index, offset in enumerate(DIRECTIONS)}
@@ -130,13 +131,15 @@
 
 
 def kernel(
-    n_lat, n_lon, forcing, search, depth_in, mask_in, fold_map, out_height, out_residual,
+    n_lat, n_lon, forcing_hbm, search_hbm, depth_hbm, mask_hbm, fold_hbm,
+    out_height, out_residual, forcing, search, depth_in, mask_in, fold_map,
     depth, depth_e, depth_w, root, root_e, root_w, weights, basis, basis_halo,
     row_north, row_south, fold_rows, packed, got_north, got_south, got_east, got_west,
-    corners, fold_all, dots, sums_lat, sums_lon, moment_rows,
+    corners, fold_all, dots, sums_lat, sums_lon, sums_all, moment_rows, load_sem,
     near_send, near_recv, fold_send, fold_recv, lat_send, lat_recv, lon_send, lon_recv,
+    all_send, all_recv,
 ):
-    rows, width = forcing.shape
+    rows, width = forcing_hbm.shape
     lat, lon = lax.axis_index("lat"), lax.axis_index("lon")
     top = n_lat - 1
     north, south = lax.rem(lat + 1, n_lat), lax.rem(lat + n_lat - 1, n_lat)
@@ -150,14 +153,33 @@
     def greet(place):
         pl.semaphore_signal(barrier, inc=1, device_id=place, device_id_type=MESH)
 
-    for d in range(1, n_lat):
-        greet((lax.rem(lat + d, n_lat), lon))
-    for d in range(1, n_lon):
-        greet((lat, lax.rem(lon + d, n_lon)))
-
-    for place in ((north, east), (north, west), (south, east), (south, west)):
-        greet(place)
-
+    loads = [
+        pltpu.make_async_copy(source, target, load_sem.at[index])
+        for index, (source, target) in enumerate(
+            ((mask_hbm, mask_in), (depth_hbm, depth_in), (search_hbm, search),
+             (forcing_hbm, forcing), (fold_hbm, fold_map))
+        )
+    ]
+    for load in loads:
+        load.start()
+    direct = n_lat * n_lon <= DIRECT_LIMIT
+    everyone = [(a, b) for a in range(n_lat) for b in range(n_lon) if a or b]
+    everyone.sort(key=lambda d: -min(d[0], n_lat - d[0]) - min(d[1], n_lon - d[1]))
+    if direct:
+        for a, b in everyone:
+            greet((lax.rem(lat + a, n_lat), lax.rem(lon + b, n_lon)))
+        greeted = len(everyone)
+    else:
+        for d in range(1, n_lat):
+            greet((lax.rem(lat + d, n_lat), lon))
+        for d in range(1, n_lon):
+            greet((lat, lax.rem(lon + d, n_lon)))
+        for place in ((north, east), (north, west), (south, east), (south, west)):
+            greet(place)
+        greeted = n_lat - 1 + n_lon - 1 + 4
+
+    for load in loads:
+        load.wait()
     lane_group = lax.broadcasted_iota(jnp.int32, (group_rows, width), 1)
     west_edge = east_edge = None
     for g in range(n_groups):
@@ -202,7 +224,7 @@
             fold_rows[24 + r : 25 + r, :] = basis[STEPS + 1, last - 1 - r : last - r, :]
         fold_all[lon] = fold_rows[...]
 
-    pl.semaphore_wait(barrier, n_lat - 1 + n_lon - 1 + 4)
+    pl.semaphore_wait(barrier, greeted)
 
     def near(index, source, target, place):
         return pltpu.make_async_remote_copy(
@@ -451,29 +473,50 @@
             dots[order_of()[key]] = dot_sums.pop(key)
 
     number = len(order_of())
+    pending = []
     lane = lax.broadcasted_iota(jnp.int32, (8, width), 1)
+    home = lane - lax.broadcasted_iota(jnp.int32, (8, width), 0)
     message = jnp.zeros((8, width), jnp.float32)
     for g in range(number // 8):
         grouped = fold_sublanes([dots[8 * g + s] for s in range(8)])
-        message = jnp.where(lane == g, jnp.sum(grouped, axis=1, keepdims=True), message)
-    for slots, size, along_lat, send_sem, recv_sem in (
-        (sums_lat, n_lat, True, lat_send, lat_recv),
-        (sums_lon, n_lon, False, lon_send, lon_recv),
-    ):
-        me = lat if along_lat else lon
-        slots[me] = message
-        copies = spread(slots.at[me], slots, send_sem, recv_sem, along_lat)
+        message = jnp.where(home == 8 * g, jnp.sum(grouped, axis=1, keepdims=True), message)
+    message = jnp.sum(message, axis=0, keepdims=True)
+    if direct:
+        me = lat * n_lon + lon
+        sums_all[me] = message
+        copies = [
+            pltpu.make_async_remote_copy(
+                src_ref=sums_all.at[me], dst_ref=sums_all.at[me], send_sem=all_send.at[index],
+                recv_sem=all_recv.at[index],
+                device_id=(lax.rem(lat + a, n_lat), lax.rem(lon + b, n_lon)),
+                device_id_type=MESH,
+            )
+            for index, (a, b) in enumerate(everyone)
+        ]
+        rounds = ((sums_all, n_lat * n_lon, copies),)
+    else:
+        rounds = (
+            (sums_lat, n_lat, None, lat, True, lat_send, lat_recv),
+            (sums_lon, n_lon, None, lon, False, lon_send, lon_recv),
+        )
+    for slots, size, copies, *rest in rounds:
+        if copies is None:
+            me, along_lat, send_sem, recv_sem = rest
+            slots[me] = message
+            copies = spread(slots.at[me], slots, send_sem, recv_sem, along_lat)
         for copy in copies:
             copy.start()
         for copy in copies:
             copy.wait_recv()
-        message = slots[0]
-        for index in range(1, size):
-            message = message + slots[index]
-        for copy in copies:
-            copy.wait_send()
+        terms = [slots[index] for index in range(size)]
+        while len(terms) > 1:
+            odd = terms[len(terms) // 2 * 2 :]
+            terms = [x + y for x, y in zip(terms[0::2], terms[1::2])] + odd
+        message = terms[0]
+        pending.extend(copies)
+    message = jnp.broadcast_to(message, (8, width))
     for g in range(number // 8):
-        picked = jnp.sum(jnp.where(lane == g, message, 0.0), axis=1, keepdims=True)
+        picked = jnp.sum(jnp.where(home == 8 * g, message, 0.0), axis=1, keepdims=True)
         moment_rows[8 * g : 8 * g + 8, :] = jnp.broadcast_to(picked, (8, width))
     moments = {}
     for kind in (("p", "p"), ("p", "r"), ("r", "r")):
@@ -493,6 +536,8 @@
                 total = term if total is None else total + term
             out[at : at + 8, :] = total
 
+    for copy in pending:
+        copy.wait_send()
     to_east.wait_send()
     to_west.wait_send()
 
@@ -520,22 +565,31 @@
     return {key: index for index, key in enumerate(keys)}
 
 
+def hand_over(height, residual, out_height, out_residual):
+    out_height[...] = height[...]
+    out_residual[...] = residual[...]
+
+
 def per_device(n_lat, n_lon, forcing, search_direction, ocean_depth, land_mask, fold_map):
     rows, width = forcing.shape
     tall = rows + 2 * PAD
     f32 = jnp.float32
+    own = pltpu.VMEM((rows, width), f32)
     pair = pltpu.VMEM((2, tall, width), f32)
     edge = pltpu.VMEM((32, width), f32)
     group_rows = rows * GROUP // width
     strip = pltpu.VMEM((group_rows, width), f32)
+    everyone = n_lat * n_lon if n_lat * n_lon <= DIRECT_LIMIT else 2
     dma = pltpu.SemaphoreType.DMA
     block = pl.BlockSpec(memory_space=pltpu.VMEM)
-    return pl.pallas_call(
+    outs = pl.pallas_call(
         functools.partial(kernel, n_lat, n_lon),
         out_shape=[jax.ShapeDtypeStruct((rows, width), f32)] * 2,
-        in_specs=[block] * 4 + [pl.BlockSpec(memory_space=pltpu.SMEM)],
+        in_specs=[pl.BlockSpec(memory_space=pl.ANY)] * 5,
         out_specs=[block] * 2,
         scratch_shapes=[
+            own, own, own, pltpu.VMEM((rows, width), jnp.int32),
+            pltpu.SMEM(fold_map.shape, jnp.int32),
             pair, pair, pair, pair, pair, pair,
             pltpu.VMEM((8, 2, tall, width), f32),
             pltpu.VMEM((2 * STEPS + 1, tall, width), f32),
@@ -546,17 +600,27 @@
             pltpu.VMEM((4, 16, width), f32),
             pltpu.VMEM((n_lon, 32, width), f32),
             pltpu.VMEM((6 * STEPS, 8, width), f32),
-            pltpu.VMEM((n_lat, 8, width), f32),
-            pltpu.VMEM((n_lon, 8, width), f32),
+            pltpu.VMEM((n_lat, 1, width), f32),
+            pltpu.VMEM((n_lon, 1, width), f32),
+            pltpu.VMEM((everyone, 1, width), f32),
             pltpu.VMEM((6 * STEPS, width), f32),
+            dma((5,)),
             dma((8,)), dma((8,)),
             dma((n_lon - 1,)), dma((n_lon - 1,)),
             dma((n_lat - 1,)), dma((n_lat - 1,)),
             dma((n_lon - 1,)), dma((n_lon - 1,)),
+            dma((everyone - 1,)), dma((everyone - 1,)),
         ],
         compiler_params=pltpu.CompilerParams(collective_id=0, has_side_effects=True),
         name="tripole_cg",
     )(forcing, search_direction, ocean_depth, land_mask, fold_map)
+    return pl.pallas_call(
+        hand_over,
+        out_shape=[jax.ShapeDtypeStruct((rows, width), f32)] * 2,
+        in_specs=[block] * 2,
+        out_specs=[block] * 2,
+        name="hand_over",
+    )(*outs)
 
 
 def solution(mesh):

time: 27.4 us -> 24.4 us (0.89)
  local copies, waits for them, and re-layouts: 2.2 us -> 0 us
  Pallas kernels: 24.3 us -> 23.6 us
    pallas_call x1, Pallas kernels: 24.3 us -> 22 us  [per_device(): pl.pallas_call(functools.partial(kernel, n_lat, n_lon), out_shape=[jax.Sh...]
    unnamed x4 -> x0, local copies, waits for them, and re-layouts: 2.2 us -> none
    pallas_call x0 -> x1, Pallas kernels: none -> 1.6 us  [per_device(): pl.pallas_call(hand_over, out_shape=[jax.ShapeDtypeStruct((rows, width),...]
where the time goes in v2:
time: 24.4 us; the launch traced here: 24.2 us
  Pallas kernels  23.6 us (97%)
  between operations  0.64 us (3%)
    pallas_call x1, Pallas kernels, per_device(): pl.pallas_call(functools.partial(kernel, n_lat, n_lon), out_shape=[jax.Sh...  22 us
    pallas_call x1, Pallas kernels, per_device(): pl.pallas_call(hand_over, out_shape=[jax.ShapeDtypeStruct((rows, width),...  1.6 us

profile of v2, /device:TPU:0, one launch (start us, length us, event | category | flops | bytes accessed | tf_op | source)
XLA Modules:
  0.0 24.2 jit_solution(11537598091388653392)
XLA Ops:
  0.6 22.0 %tripole_cg.1 = (f32[160,128]{1,0:T(8,128)}, f32[160,128]{1,0:T(8,128)}) custom-call(f32[160,128]{1,0:T(8,128)} %forcing_hbm.1, f32[160,128]{1,0:T(8,128)} %search_hbm.1, f32[160,128]{1,0:T(8,128)} %depth_hbm.1, s32[160,128]{1,0:T(8,128)} %mask_hbm.1, s32[1024]{0:T(1024)} %fold_hbm.1), custom_call_target="tpu_custom_call" | custom-call | tf_op jit(solution)/shard_map/tripole_cg/pallas_call | solution.py:585
  22.6 1.6 %hand_over.1 = (f32[160,128]{1,0:T(8,128)}, f32[160,128]{1,0:T(8,128)}) custom-call(f32[160,128]{1,0:T(8,128)} %get-tuple-element.4.height, f32[160,128]{1,0:T(8,128)} %get-tuple-element.5.residual), custom_call_target="tpu_custom_call" | custom-call | tf_op jit(solution)/shard_map/hand_over/pallas_call | solution.py:617
